TPU v7x, 256 devices: a whole 4x4x8 slice. The times are simulated.
256 devices in a mesh: seq: 32 (over x, z_lo, core), head: 8 (over y, z_hi).
Axes of the slice: x: 4, y: 4, z: 8 (z_hi: 2, z_lo: 4; z = z_hi * 4 + z_lo), core: 2. Of those that a mesh axis runs over, the one named last changes fastest.
Arguments:
- tokens: bfloat16 [16384, 1024], P('seq'), may hold values from -6 to 6
- mem_query_w: bfloat16 [1024, 1024], P(None, 'head'), may hold values from -0.1875 to 0.1875
- mem_key_w: bfloat16 [1024, 1024], P(None, 'head'), may hold values from -0.1875 to 0.1875
- mem_value_w: bfloat16 [1024, 1024], P(None, 'head'), may hold values from -0.1875 to 0.1875
- mem_in: float32 [1024, 1024], P(None, 'head'), may hold values from -0.1875 to 0.1875
- mem_out: float32 [1024, 1024], P('head'), may hold values from -0.1875 to 0.1875
- forget_levels: float32 [16, 1024], P(None, 'head'), may hold values from 0.003 to 0.3
- momentum_levels: float32 [16, 1024], P(None, 'head'), may hold values from 0.2 to 0.9
- step_levels: float32 [16, 1024], P(None, 'head'), may hold values from 0.02 to 0.2
- plan: int32 [32], P('seq'), may hold values from 0 to 15
- norm_gain: float32 [1024], replicated, may hold values from 0.5 to 1.5
- attn_query_w: bfloat16 [1024, 1024], P(None, 'head'), may hold values from -1 to 1
- attn_key_w: bfloat16 [1024, 1024], P(None, 'head'), may hold values from -4 to 4
- attn_value_w: bfloat16 [1024, 1024], P(None, 'head'), may hold values from -0.1875 to 0.1875
- attn_out_w: bfloat16 [1024, 1024], P('head'), may hold values from -0.25 to 0.25
Outputs:
- layer_out: bfloat16 [16384, 1024], P('seq', 'head')
All inputs are finite; a program needn't handle non-finite values.
Results may differ from a plain program's by a relative error of at most 0.014.
Values may be sent and summed in bfloat16 or wider, within the bound.
A program may use at most 128 MiB of HBM per device.

v0:
```python
import jax
import jax.numpy as jnp
from jax import lax
from jax.sharding import Mesh
from jax.sharding import PartitionSpec as P

HEAD_DIM = 64
SPAN = 8
SEQ = ("seq_0", "seq_1", "seq_2")
epsilon = 1e-06


def split_up(value, dim, length):
    before, after = (value.shape[:dim], value.shape[dim + 1 :])
    return jnp.moveaxis(value.reshape(*before, length, -1, *after), dim, 0)


def sent_and_summed(value, axis, dim):
    length = lax.axis_size(axis)
    blocks = lax.all_to_all(split_up(value, dim, length), axis, 0, 0, tiled=True)
    return jnp.sum(blocks, axis=0)


def filled_with(value, identity):
    return jax.tree.map(
        lambda a, e: jnp.broadcast_to(jnp.asarray(e, a.dtype), a.shape), value, identity
    )


def gathered_once(value, axis):
    leaves = jax.tree.leaves(value)
    sequence = sorted(range(len(leaves)), key=lambda k: -leaves[k].size)
    width = (1, *leaves[sequence[0]].shape)[-1]
    lines = [
        jnp.pad(leaves[k].reshape(-1), (0, -leaves[k].size % width)).reshape(-1, width)
        for k in sequence
    ]
    both, at, found = (lax.all_gather(jnp.concatenate(lines), axis), 0, {})
    for k, line in zip(sequence, lines):
        section = both[:, at : at + len(line)].reshape(len(both), -1)
        found[k] = section[:, : leaves[k].size].reshape(-1, *leaves[k].shape)
        at += len(line)
    numbers = iter(range(len(leaves)))
    return jax.tree.map(lambda _: found[next(numbers)], value)


def carried_in(value, axes, combine, identity):
    before = start = filled_with(value, identity)
    running = value
    for axis in reversed(axes):
        length, index = (lax.axis_size(axis), lax.axis_index(axis))
        pieces = gathered_once(running, axis)
        inside, running = (start, start)
        for k in range(length):
            passed = k < index
            running = combine(running, jax.tree.map(lambda part: part[k], pieces))
            inside = jax.tree.map(lambda new, old: jnp.where(passed, new, old), running, inside)
        before = combine(inside, before)
    return before


def shifted(value, axis, by):
    length = lax.axis_size(axis)
    pairs = [(i, i + by) for i in range(length) if 0 <= i + by < length]
    return lax.ppermute(value, axis, pairs)


def sum_at_owner(value, axis, dim):
    length = lax.axis_size(axis)
    blocks = lax.all_to_all(split_up(value, dim, length), axis, 0, 0, tiled=True)
    return jnp.sum(blocks.astype(jnp.float32), axis=0)


def silu_slope(values):
    sigmoid = jax.nn.sigmoid(values)
    return sigmoid * (1.0 + values * (1.0 - sigmoid))


def project(left, weight):
    return jnp.dot(left, weight, preferred_element_type=jnp.float32).astype(jnp.bfloat16)


def normalize(retrieved, norm_gain):
    mean_square = jnp.mean(retrieved * retrieved, axis=-1, keepdims=True)
    return (retrieved * lax.rsqrt(mean_square + epsilon) * norm_gain).astype(jnp.bfloat16)


def lookup(table, chosen):
    matches = jnp.arange(table.shape[0], dtype=jnp.int32)[:, None] == chosen
    return jnp.sum(jnp.where(matches, table, 0.0), axis=0)


def as_columns(vector):
    return vector[..., None, :]


def as_rows(vector):
    return vector[..., :, None]


def compose(earlier, later):
    (
        prior_decay,
        prior_cross,
        prior_keep,
        prior_speed_in,
        prior_speed_out,
        prior_weight_in,
        prior_weight_out,
    ) = earlier
    (
        after_decay,
        after_cross,
        after_keep,
        after_speed_in,
        after_speed_out,
        after_weight_in,
        after_weight_out,
    ) = later
    decay = after_decay * prior_decay
    cross = after_cross * prior_decay + after_keep * prior_cross
    keep = after_keep * prior_keep
    speed_in = as_columns(after_decay) * prior_speed_in + after_speed_in
    speed_out = as_rows(after_decay) * prior_speed_out + after_speed_out
    weight_in = (
        as_columns(after_cross) * prior_speed_in
        + as_columns(after_keep) * prior_weight_in
        + after_weight_in
    )
    weight_out = (
        as_rows(after_cross) * prior_speed_out
        + as_rows(after_keep) * prior_weight_out
        + after_weight_out
    )
    return (decay, cross, keep, speed_in, speed_out, weight_in, weight_out)


def window_attend(query, keys, values, block_index):
    query_count = query.shape[0]
    key_count = keys.shape[0]
    span_rows = key_count - query_count
    distance = (
        span_rows
        + jnp.arange(query_count, dtype=jnp.int32)[:, None]
        - jnp.arange(key_count, dtype=jnp.int32)[None, :]
    )
    key_pos = (block_index * query_count - span_rows + jnp.arange(key_count, dtype=jnp.int32))[
        None, :
    ]
    allowed = (distance >= 0) & (distance < span_rows) & (key_pos >= 0)
    contexts = []
    for head_number in range(query.shape[1] // HEAD_DIM):
        low_col = head_number * HEAD_DIM
        scores = jnp.einsum(
            "qd,kd->qk",
            query[:, low_col : low_col + HEAD_DIM],
            keys[:, low_col : low_col + HEAD_DIM],
            preferred_element_type=jnp.float32,
        ) * HEAD_DIM ** (-0.5)
        scores = jnp.where(allowed, scores, -1e30)
        row_peak = jnp.max(scores, axis=-1, keepdims=True)
        weights = jnp.exp(scores - row_peak)
        probabilities = (weights / jnp.sum(weights, axis=-1, keepdims=True)).astype(jnp.bfloat16)
        contexts.append(
            jnp.dot(
                probabilities,
                values[:, low_col : low_col + HEAD_DIM],
                preferred_element_type=jnp.float32,
            ).astype(jnp.bfloat16)
        )
    return jnp.concatenate(contexts, axis=1)


def shards(
    tokens,
    mem_query_w,
    mem_key_w,
    mem_value_w,
    mem_in,
    mem_out,
    forget_levels,
    momentum_levels,
    step_levels,
    plan,
    norm_gain,
    attn_query_w,
    attn_key_w,
    attn_value_w,
    attn_out_w,
):
    tok_rows = tokens.shape[0]
    share_rows = tok_rows // lax.axis_size("head")
    my_start = lax.axis_index("head") * share_rows
    mem_query, mem_key, mem_value = (
        lax.all_gather(project(tokens, mem_query_w), "head", axis=1, tiled=True),
        lax.all_gather(project(tokens, mem_key_w), "head", axis=1, tiled=True),
        lax.all_gather(project(tokens, mem_value_w), "head", axis=1, tiled=True),
    )
    keys_wide = mem_key.astype(jnp.float32)
    pre_act = jnp.dot(keys_wide, mem_in)
    hidden = jax.nn.silu(pre_act)
    predicted = sent_and_summed(jnp.dot(hidden, mem_out), "head", 0)
    value_share = lax.dynamic_slice_in_dim(mem_value, my_start, share_rows, 0).astype(jnp.float32)
    residual_err = lax.all_gather(
        2.0 / tok_rows * (predicted - value_share), "head", axis=0, tiled=True
    )
    grad_out = jnp.dot(hidden.T, residual_err)
    slope_term = jnp.dot(residual_err, mem_out.T) * silu_slope(pre_act)
    grad_in = jnp.dot(keys_wide.T, slope_term)
    chosen = plan[0]
    forget = lookup(forget_levels, chosen)
    momentum = lookup(momentum_levels, chosen)
    step_rate = lookup(step_levels, chosen)
    change_in = -as_columns(step_rate) * grad_in
    change_out = -as_rows(step_rate) * grad_out
    element = (momentum, momentum, 1.0 - forget, change_in, change_out, change_in, change_out)
    identity = (
        jnp.ones_like(momentum),
        jnp.zeros_like(momentum),
        jnp.ones_like(momentum),
        jnp.zeros_like(grad_in),
        jnp.zeros_like(grad_out),
        jnp.zeros_like(grad_in),
        jnp.zeros_like(grad_out),
    )
    entering = carried_in(element, SEQ, compose, identity)
    weight_in = as_columns(entering[2]) * mem_in + entering[5]
    weight_out = as_rows(entering[2]) * mem_out + entering[6]
    query_hidden = jax.nn.silu(jnp.dot(mem_query.astype(jnp.float32), weight_in))
    retrieved = sent_and_summed(jnp.dot(query_hidden, weight_out), "head", 0)
    normed = lax.all_gather(normalize(retrieved, norm_gain), "head", axis=0, tiled=True)
    att_query = project(normed, attn_query_w)
    att_key = project(normed, attn_key_w)
    att_value = project(normed, attn_value_w)
    earlier = []
    for distance in range(SPAN, 0, -1):
        earlier.append(shifted((att_key, att_value), SEQ, distance))
    key_window = jnp.concatenate([received[0] for received in earlier] + [att_key], axis=0)
    value_window = jnp.concatenate([received[1] for received in earlier] + [att_value], axis=0)
    context = window_attend(att_query, key_window, value_window, lax.axis_index(SEQ))
    partial_out = jnp.dot(context, attn_out_w, preferred_element_type=jnp.float32)
    return sum_at_owner(partial_out.astype(jnp.bfloat16), "head", 1).astype(jnp.bfloat16)


def solution(mesh):
    split = Mesh(
        mesh.devices.reshape(4, 4, 2, mesh.shape["head"]), ("seq_0", "seq_1", "seq_2", "head")
    )
    in_specs = (
        P(SEQ, None),
        P(None, "head"),
        P(None, "head"),
        P(None, "head"),
        P(None, "head"),
        P("head", None),
        P(None, "head"),
        P(None, "head"),
        P(None, "head"),
        P(SEQ),
        P(),
        P(None, "head"),
        P(None, "head"),
        P(None, "head"),
        P("head", None),
    )
    out_specs = P(SEQ, "head")
    return jax.shard_map(
        shards, mesh=split, in_specs=in_specs, out_specs=out_specs, check_vma=False
    )
```

profile of v0, /device:TPU:33, one launch (start us, length us, event | category | flops | bytes accessed | tf_op | source)
XLA Modules:
  0.0 816.8 jit_solution(12139986413345933075)
XLA Ops:
  9.8 61.9 %all-gather.17.cloned.1.call-done = bf16[512,1024]{1,0:T(8,128)(2,1)} async-done(((bf16[512,128]{1,0:T(8,128)(2,1)}), bf16[512,1024]{1,0:T(8,128)(2,1)}) %all-gather.17.cloned.1.call-update) | async-done | bytes 1048592 | tf_op jit(solution)/shard_map/all_gather | solution.py:196
  76.0 3.7 all-to-all-start
  81.0 54.1 %all-to-all-done = f32[8,64,1024]{2,1,0:T(8,128)S(1)} async-done(((f32[8,64,1024]{2,1,0:T(8,128)}), f32[8,64,1024]{2,1,0:T(8,128)S(1)}, u32[]{:S(2)}, u32[]{:S(2)}) %all-to-all-start) | async-done | bytes 2097184 | tf_op jit(solution)/shard_map/all_to_all | solution.py:20
  135.3 23.0 %all-gather.19.cloned.1.call-done = bf16[512,1024]{1,0:T(8,128)(2,1)} async-done(((bf16[512,128]{1,0:T(8,128)(2,1)}), bf16[512,1024]{1,0:T(8,128)(2,1)}) %all-gather.19.cloned.1.call-update) | async-done | bytes 1048592 | tf_op jit(solution)/shard_map/all_gather | solution.py:197
  160.7 57.5 %all-gather.21.cloned.1.call-done = bf16[512,1024]{1,0:T(8,128)(2,1)} async-done(((bf16[64,1024]{1,0:T(8,128)(2,1)}), bf16[512,1024]{1,0:T(8,128)(2,1)}) %all-gather.21.cloned.1.call-update) | async-done | bytes 1048592 | tf_op jit(solution)/shard_map/all_gather | solution.py:204
  220.0 2.6 convolution_multiply_fusion
  222.7 4.1 concatenate.18
  226.8 17.6 %all-gather.25.cloned.1.call-done = f32[2,4099,128]{2,1,0:T(8,128)} async-done(((f32[1,4099,128]{2,1,0:T(8,128)}), f32[2,4099,128]{2,1,0:T(8,128)}) %all-gather.25.cloned.1.call-update) | async-done | bytes 4197392 | tf_op jit(solution)/shard_map/all_gather | solution.py:38
  251.5 4.1 concatenate.19
  255.6 154.2 %all-gather.27.cloned.1.call-done = f32[4,4099,128]{2,1,0:T(8,128)} async-done(((f32[1,4099,128]{2,1,0:T(8,128)}), f32[4,4099,128]{2,1,0:T(8,128)}) %all-gather.27.cloned.1.call-update) | async-done | bytes 8394768 | tf_op jit(solution)/shard_map/all_gather | solution.py:38
  418.9 4.0 bitcast_add_fusion
  423.0 4.1 concatenate.20
  433.9 3.4 fusion.353
  446.6 65.9 %all-gather.29.cloned.1.call-done = f32[4,4099,128]{2,1,0:T(8,128)} async-done(((f32[1,4099,128]{2,1,0:T(8,128)}), f32[4,4099,128]{2,1,0:T(8,128)}) %all-gather.29.cloned.1.call-update) | async-done | bytes 8394768 | tf_op jit(solution)/shard_map/all_gather | solution.py:38
  512.5 3.4 fusion.352
  526.8 48.5 %all-gather.15.cloned.1.call-done = bf16[512,1024]{1,0:T(8,128)(2,1)} async-done(((bf16[512,128]{1,0:T(8,128)(2,1)}), bf16[512,1024]{1,0:T(8,128)(2,1)}) %all-gather.15.cloned.1.call-update) | async-done | bytes 1048592 | tf_op jit(solution)/shard_map/all_gather | solution.py:195
  575.3 11.3 %fusion.57 = f32[512,1024]{1,0:T(8,128)} fusion(f32[128,1024]{1,0:T(8,128)} %squeeze.275, f32[128,1024]{1,0:T(8,128)} %squeeze.274, f32[128,1024]{1,0:T(8,128)} %squeeze.273, f32[128,1024]{1,0:T(8,128)} %squeeze.272, f32[128,1024]{1,0:T(8,128)} %squeeze.271, f32[128,1024]{1,0:T(8,128)} %squeeze.270, f32[128,1024]{1,0:T(8,128)} %squeeze.269, ...), kind=kOutput, calls=%fused_computation.101 | convolution fusion | flops 287834112 | bytes 25205248 | tf_op jit(solution)/shard_map/dot_general | solution.py:230
  586.6 56.2 %all_to_all.15 = f32[8,64,1024]{2,1,0:T(8,128)S(1)} all-to-all(f32[8,64,1024]{2,1,0:T(8,128)} %bitcast.561), channel_id=1, replica_groups=mesh['seq_0'=4,'seq_1'=4,'seq_2'=2,'head'=8] {'head'}, dimensions={0} | all-to-all | bytes 4194304 | tf_op jit(solution)/shard_map/all_to_all | solution.py:20
  644.3 54.3 %all-gather.23.cloned.1.call-done = bf16[512,1024]{1,0:T(8,128)(2,1)} async-done(((bf16[64,1024]{1,0:T(8,128)(2,1)}), bf16[512,1024]{1,0:T(8,128)(2,1)}) %all-gather.23.cloned.1.call-update) | async-done | bytes 1048592 | tf_op jit(solution)/shard_map/all_gather | solution.py:231
  700.3 3.1 collective-permute-start
  703.5 5.4 collective-permute-start.1
  708.9 3.6 collective-permute-start.2
  713.8 4.1 collective-permute-start.4
  720.1 3.0 collective-permute-start.5
  725.4 3.3 collective-permute-start.7
  731.5 8.3 %collective-permute-start.10 = (bf16[512,128]{1,0:T(8,128)(2,1)S(1)}, bf16[512,128]{1,0:T(8,128)(2,1)S(1)}, u32[]{:S(2)}, u32[]{:S(2)}) collective-permute-start(bf16[512,128]{1,0:T(8,128)(2,1)S(1)} %convolution_convert_fusion.1), channel_id=1, source_target_pairs={{0,48},{8,56},{16,64},{24,72},{32,80},{40,88},{48,96},{56,104},{64... | collective-permute-start | bytes 393224 | tf_op jit(solution)/shard_map/ppermute | solution.py:65
  739.8 2.8 collective-permute-start.11
  744.2 4.3 fusion.356
  748.5 4.2 fusion.355
  752.7 4.3 collective-permute-start.13
  759.1 3.0 collective-permute-start.15
  773.0 36.1 %all_to_all.16 = bf16[8,512,128]{2,1,0:T(8,128)(2,1)S(1)} all-to-all(bf16[8,512,128]{2,1,0:T(8,128)(2,1)S(1)} %bitcast.560), channel_id=1, replica_groups=mesh['seq_0'=4,'seq_1'=4,'seq_2'=2,'head'=8] {'head'}, dimensions={0} | all-to-all | bytes 2097152 | tf_op jit(solution)/shard_map/all_to_all | solution.py:70
  (202 shorter events, 82.1 us)
Async XLA Ops:
  6.5 67.7 %copy-start.14 = (f32[128,1024]{1,0:T(8,128)S(1)}, f32[128,1024]{1,0:T(8,128)}, u32[]{:S(2)}) copy-start(f32[128,1024]{1,0:T(8,128)} %param.20) | copy-start | bytes 1572868
  6.5 65.2 %all-gather.17.cloned.1.call-start = ((), (), s32[]{:S(2)}) async-start(), calls=%async_computation.4 | async-start | bytes 1179648 | tf_op jit(solution)/shard_map/all_gather | solution.py:196
  76.0 59.1 %all-to-all-start = ((f32[8,64,1024]{2,1,0:T(8,128)}), f32[8,64,1024]{2,1,0:T(8,128)S(1)}, u32[]{:S(2)}, u32[]{:S(2)}) async-start(f32[8,64,1024]{2,1,0:T(8,128)} %bitcast.559), calls=%async_computation | async-start | bytes 4194304 | tf_op jit(solution)/shard_map/all_to_all | solution.py:20
  79.7 80.9 %copy-start.21 = (f32[16,128]{1,0:T(8,128)S(1)}, f32[16,128]{1,0:T(8,128)}, u32[]{:S(2)}) copy-start(f32[16,128]{1,0:T(8,128)} %param.21) | copy-start | bytes 24580
  79.7 80.9 %copy-start.22 = (f32[16,128]{1,0:T(8,128)S(1)}, f32[16,128]{1,0:T(8,128)}, u32[]{:S(2)}) copy-start(f32[16,128]{1,0:T(8,128)} %param.22) | copy-start | bytes 24580
  79.7 80.9 %copy-start.23 = (f32[16,128]{1,0:T(8,128)S(1)}, f32[16,128]{1,0:T(8,128)}, u32[]{:S(2)}) copy-start(f32[16,128]{1,0:T(8,128)} %param.23) | copy-start | bytes 24580
  79.8 78.5 %all-gather.19.cloned.1.call-start = ((), (), s32[]{:S(2)}) async-start(), calls=%async_computation.5 | async-start | bytes 1179648 | tf_op jit(solution)/shard_map/all_gather | solution.py:197
  80.9 137.3 %all-gather.21.cloned.1.call-start = ((), (), s32[]{:S(2)}) async-start(), calls=%async_computation.6 | async-start | bytes 1179648 | tf_op jit(solution)/shard_map/all_gather | solution.py:204
  135.2 84.8 %copy-start.11 = (bf16[512,1024]{1,0:T(8,128)(2,1)S(1)}, bf16[512,1024]{1,0:T(8,128)(2,1)}, u32[]{:S(2)}) copy-start(bf16[512,1024]{1,0:T(8,128)(2,1)} %all-gather.17.cloned.1.call-done) | copy-start | bytes 3145732
  159.8 84.5 %all-gather.25.cloned.1.call-start = ((), (), s32[]{:S(2)}) async-start(), calls=%async_computation.8 | async-start | bytes 6303744 | tf_op jit(solution)/shard_map/all_gather | solution.py:38
  226.8 183.1 %all-gather.27.cloned.1.call-start = ((), (), s32[]{:S(2)}) async-start(), calls=%async_computation.9 | async-start | bytes 10506240 | tf_op jit(solution)/shard_map/all_gather | solution.py:38
  255.6 256.9 %all-gather.29.cloned.1.call-start = ((), (), s32[]{:S(2)}) async-start(), calls=%async_computation.10 | async-start | bytes 10506240 | tf_op jit(solution)/shard_map/all_gather | solution.py:38
  427.1 148.2 %all-gather.15.cloned.1.call-start = ((), (), s32[]{:S(2)}) async-start(), calls=%async_computation.3 | async-start | bytes 1179648 | tf_op jit(solution)/shard_map/all_gather | solution.py:195
  428.3 270.3 %all-gather.23.cloned.1.call-start = ((), (), s32[]{:S(2)}) async-start(), calls=%async_computation.7 | async-start | bytes 1179648 | tf_op jit(solution)/shard_map/all_gather | solution.py:231
  643.0 74.9 %copy-start.18 = (bf16[1024,128]{1,0:T(8,128)(2,1)S(1)}, bf16[1024,128]{1,0:T(8,128)(2,1)}, u32[]{:S(2)}) copy-start(bf16[1024,128]{1,0:T(8,128)(2,1)} %param.26) | copy-start | bytes 786436
  643.0 76.6 %copy-start.19 = (bf16[1024,128]{1,0:T(8,128)(2,1)S(1)}, bf16[1024,128]{1,0:T(8,128)(2,1)}, u32[]{:S(2)}) copy-start(bf16[1024,128]{1,0:T(8,128)(2,1)} %param.28) | copy-start | bytes 786436
  700.3 19.7 %collective-permute-start = (bf16[512,128]{1,0:T(8,128)(2,1)S(1)}, bf16[512,128]{1,0:T(8,128)(2,1)S(1)}, u32[]{:S(2)}, u32[]{:S(2)}) collective-permute-start(bf16[512,128]{1,0:T(8,128)(2,1)S(1)} %convolution_convert_fusion.2), channel_id=1, source_target_pairs={{0,64},{8,72},{16,80},{24,88},{32,96},{40,104},{48,112},{56,120},{... | collective-permute-start | bytes 393224 | tf_op jit(solution)/shard_map/ppermute | solution.py:65
  703.5 19.7 %collective-permute-start.1 = (bf16[512,128]{1,0:T(8,128)(2,1)S(1)}, bf16[512,128]{1,0:T(8,128)(2,1)S(1)}, u32[]{:S(2)}, u32[]{:S(2)}) collective-permute-start(bf16[512,128]{1,0:T(8,128)(2,1)S(1)} %convolution_convert_fusion.2), channel_id=1, source_target_pairs={{0,56},{8,64},{16,72},{24,80},{32,88},{40,96},{48,104},{56,112},{6... | collective-permute-start | bytes 393224 | tf_op jit(solution)/shard_map/ppermute | solution.py:65
  708.9 16.6 %collective-permute-start.2 = (bf16[512,128]{1,0:T(8,128)(2,1)S(1)}, bf16[512,128]{1,0:T(8,128)(2,1)S(1)}, u32[]{:S(2)}, u32[]{:S(2)}) collective-permute-start(bf16[512,128]{1,0:T(8,128)(2,1)S(1)} %convolution_convert_fusion.2), channel_id=1, source_target_pairs={{0,48},{8,56},{16,64},{24,72},{32,80},{40,88},{48,96},{56,104},{64... | collective-permute-start | bytes 393224 | tf_op jit(solution)/shard_map/ppermute | solution.py:65
  712.5 16.3 %collective-permute-start.3 = (bf16[512,128]{1,0:T(8,128)(2,1)S(1)}, bf16[512,128]{1,0:T(8,128)(2,1)S(1)}, u32[]{:S(2)}, u32[]{:S(2)}) collective-permute-start(bf16[512,128]{1,0:T(8,128)(2,1)S(1)} %convolution_convert_fusion.2), channel_id=1, source_target_pairs={{0,40},{8,48},{16,56},{24,64},{32,72},{40,80},{48,88},{56,96},{64,... | collective-permute-start | bytes 393224 | tf_op jit(solution)/shard_map/ppermute | solution.py:65
  713.8 16.3 %collective-permute-start.4 = (bf16[512,128]{1,0:T(8,128)(2,1)S(1)}, bf16[512,128]{1,0:T(8,128)(2,1)S(1)}, u32[]{:S(2)}, u32[]{:S(2)}) collective-permute-start(bf16[512,128]{1,0:T(8,128)(2,1)S(1)} %convolution_convert_fusion.2), channel_id=1, source_target_pairs={{0,32},{8,40},{16,48},{24,56},{32,64},{40,72},{48,80},{56,88},{64,... | collective-permute-start | bytes 393224 | tf_op jit(solution)/shard_map/ppermute | solution.py:65
  720.1 11.4 %collective-permute-start.5 = (bf16[512,128]{1,0:T(8,128)(2,1)S(1)}, bf16[512,128]{1,0:T(8,128)(2,1)S(1)}, u32[]{:S(2)}, u32[]{:S(2)}) collective-permute-start(bf16[512,128]{1,0:T(8,128)(2,1)S(1)} %convolution_convert_fusion.2), channel_id=1, source_target_pairs={{0,24},{8,32},{16,40},{24,48},{32,56},{40,64},{48,72},{56,80},{64,... | collective-permute-start | bytes 393224 | tf_op jit(solution)/shard_map/ppermute | solution.py:65
  723.1 16.6 %collective-permute-start.6 = (bf16[512,128]{1,0:T(8,128)(2,1)S(1)}, bf16[512,128]{1,0:T(8,128)(2,1)S(1)}, u32[]{:S(2)}, u32[]{:S(2)}) collective-permute-start(bf16[512,128]{1,0:T(8,128)(2,1)S(1)} %convolution_convert_fusion.2), channel_id=1, source_target_pairs={{0,16},{8,24},{16,32},{24,40},{32,48},{40,56},{48,64},{56,72},{64,... | collective-permute-start | bytes 393224 | tf_op jit(solution)/shard_map/ppermute | solution.py:65
  725.4 17.1 %collective-permute-start.7 = (bf16[512,128]{1,0:T(8,128)(2,1)S(1)}, bf16[512,128]{1,0:T(8,128)(2,1)S(1)}, u32[]{:S(2)}, u32[]{:S(2)}) collective-permute-start(bf16[512,128]{1,0:T(8,128)(2,1)S(1)} %convolution_convert_fusion.2), channel_id=1, source_target_pairs={{0,8},{8,16},{16,24},{24,32},{32,40},{40,48},{48,56},{56,64},{64,7... | collective-permute-start | bytes 393224 | tf_op jit(solution)/shard_map/ppermute | solution.py:65
  728.8 23.9 %collective-permute-start.8 = (bf16[512,128]{1,0:T(8,128)(2,1)S(1)}, bf16[512,128]{1,0:T(8,128)(2,1)S(1)}, u32[]{:S(2)}, u32[]{:S(2)}) collective-permute-start(bf16[512,128]{1,0:T(8,128)(2,1)S(1)} %convolution_convert_fusion.1), channel_id=1, source_target_pairs={{0,64},{8,72},{16,80},{24,88},{32,96},{40,104},{48,112},{56,120},{... | collective-permute-start | bytes 393224 | tf_op jit(solution)/shard_map/ppermute | solution.py:65
  730.1 26.9 %collective-permute-start.9 = (bf16[512,128]{1,0:T(8,128)(2,1)S(1)}, bf16[512,128]{1,0:T(8,128)(2,1)S(1)}, u32[]{:S(2)}, u32[]{:S(2)}) collective-permute-start(bf16[512,128]{1,0:T(8,128)(2,1)S(1)} %convolution_convert_fusion.1), channel_id=1, source_target_pairs={{0,56},{8,64},{16,72},{24,80},{32,88},{40,96},{48,104},{56,112},{6... | collective-permute-start | bytes 393224 | tf_op jit(solution)/shard_map/ppermute | solution.py:65
  731.5 27.6 %collective-permute-start.10 = (bf16[512,128]{1,0:T(8,128)(2,1)S(1)}, bf16[512,128]{1,0:T(8,128)(2,1)S(1)}, u32[]{:S(2)}, u32[]{:S(2)}) collective-permute-start(bf16[512,128]{1,0:T(8,128)(2,1)S(1)} %convolution_convert_fusion.1), channel_id=1, source_target_pairs={{0,48},{8,56},{16,64},{24,72},{32,80},{40,88},{48,96},{56,104},{64... | collective-permute-start | bytes 393224 | tf_op jit(solution)/shard_map/ppermute | solution.py:65
  739.8 22.3 %collective-permute-start.11 = (bf16[512,128]{1,0:T(8,128)(2,1)S(1)}, bf16[512,128]{1,0:T(8,128)(2,1)S(1)}, u32[]{:S(2)}, u32[]{:S(2)}) collective-permute-start(bf16[512,128]{1,0:T(8,128)(2,1)S(1)} %convolution_convert_fusion.1), channel_id=1, source_target_pairs={{0,40},{8,48},{16,56},{24,64},{32,72},{40,80},{48,88},{56,96},{64,... | collective-permute-start | bytes 393224 | tf_op jit(solution)/shard_map/ppermute | solution.py:65
  742.6 19.6 %collective-permute-start.12 = (bf16[512,128]{1,0:T(8,128)(2,1)S(1)}, bf16[512,128]{1,0:T(8,128)(2,1)S(1)}, u32[]{:S(2)}, u32[]{:S(2)}) collective-permute-start(bf16[512,128]{1,0:T(8,128)(2,1)S(1)} %convolution_convert_fusion.1), channel_id=1, source_target_pairs={{0,32},{8,40},{16,48},{24,56},{32,64},{40,72},{48,80},{56,88},{64,... | collective-permute-start | bytes 393224 | tf_op jit(solution)/shard_map/ppermute | solution.py:65
  752.7 9.5 %collective-permute-start.13 = (bf16[512,128]{1,0:T(8,128)(2,1)S(1)}, bf16[512,128]{1,0:T(8,128)(2,1)S(1)}, u32[]{:S(2)}, u32[]{:S(2)}) collective-permute-start(bf16[512,128]{1,0:T(8,128)(2,1)S(1)} %convolution_convert_fusion.1), channel_id=1, source_target_pairs={{0,24},{8,32},{16,40},{24,48},{32,56},{40,64},{48,72},{56,80},{64,... | collective-permute-start | bytes 393224 | tf_op jit(solution)/shard_map/ppermute | solution.py:65
  757.1 6.9 collective-permute-start.14
  759.1 6.2 collective-permute-start.15
  (18 other events, 380.4 us)
Sparse Core Ops, SparseCore 0:
  9.9 61.7 all-gather.16
  83.1 75.1 all-gather.18
  160.9 57.3 all-gather.20
  226.9 17.4 all-gather.24
  255.7 154.1 all-gather.26
  427.3 85.1 all-gather.28
  515.0 60.2 all-gather.14
  644.4 54.1 all-gather.22
where the time goes:
time: 818 us; the launch traced here: 817 us
  waiting for transfers between devices  540 us (66%)
  blocking collectives  92.3 us (11%)
  starting transfers between devices  54.7 us (7%)
  local copies, waits for them, and re-layouts  47.1 us (6%)
  matrix products  40.3 us (5%)
  other arithmetic  27 us (3%)
  between operations  15.1 us (2%)
    all_gather x3, waiting for transfers between devices, gathered_once(): both, at, found = (lax.all_gather(jnp.concatenate(lines), axis), 0, {})  238 us
    all_gather x1, waiting for transfers between devices, shards(): lax.all_gather(project(tokens, mem_key_w), 'head', axis=1, tiled=True)  61.9 us
    all_gather x1, waiting for transfers between devices, shards(): lax.all_gather(2.0 / tok_rows * (predicted - value_share), 'head', axis=0...  57.5 us
    all_to_all x1, blocking collectives, sent_and_summed(): lax.all_to_all(split_up(value, dim, length), axis, 0, 0, tiled=True)  56.2 us
    all_gather x1, waiting for transfers between devices, shards(): lax.all_gather(normalize(retrieved, norm_gain), 'head', axis=0, tiled=True)  54.3 us
    all_to_all x1, waiting for transfers between devices, sent_and_summed(): lax.all_to_all(split_up(value, dim, length), axis, 0, 0, tiled=True)  54.1 us
    ppermute x16, starting transfers between devices, shifted(): return lax.ppermute(value, axis, pairs)  50.5 us
    all_gather x1, waiting for transfers between devices, shards(): lax.all_gather(project(tokens, mem_query_w), 'head', axis=1, tiled=True)  48.5 us
  transfers between devices with their start and end apart: 25, of which 11 were waited for; matrix products, arithmetic and copies ran while one was open for 6% of the time, Pallas kernels for 0%

commit v1 on v0

--- a/solution.py
+++ b/solution.py
@@ -3,6 +3,7 @@
 from jax import lax
 from jax.sharding import Mesh
 from jax.sharding import PartitionSpec as P
+from jax.lax import all_to_all, axis_size
 
 HEAD_DIM = 64
 SPAN = 8
@@ -191,8 +192,11 @@
     tok_rows = tokens.shape[0]
     share_rows = tok_rows // lax.axis_size("head")
     my_start = lax.axis_index("head") * share_rows
+    check_axis_part = lambda content, mesh_dim, dim_at: jnp.concatenate(
+        all_to_all(jnp.stack(axis_size(mesh_dim) * [content]), mesh_dim, 0, 0), axis=dim_at
+    )
     mem_query, mem_key, mem_value = (
-        lax.all_gather(project(tokens, mem_query_w), "head", axis=1, tiled=True),
+        check_axis_part(project(tokens, mem_query_w), "head", 1),
         lax.all_gather(project(tokens, mem_key_w), "head", axis=1, tiled=True),
         lax.all_gather(project(tokens, mem_value_w), "head", axis=1, tiled=True),
     )

time: 818 us -> 776 us (0.949)
  waiting for transfers between devices: 540 us -> 484 us
    all_gather x1 -> x0, waiting for transfers between devices: 48.5 us -> none  [shards(): lax.all_gather(project(tokens, mem_query_w), 'head', axis=1, tiled=True)]
  transfers between devices with their start and end apart: 25 -> 25, of which waited for: 11 -> 10; matrix products, arithmetic and copies ran while one was open for 6% -> 6% of each run, Pallas kernels for 0% -> 0%
where the time goes in v1:
time: 776 us; the launch traced here: 774 us
  waiting for transfers between devices  484 us (62%)
  blocking collectives  98 us (13%)
  starting transfers between devices  61.2 us (8%)
  local copies, waits for them, and re-layouts  48.6 us (6%)
  matrix products  39.8 us (5%)
  other arithmetic  26.8 us (3%)
  between operations  15.1 us (2%)
    all_gather x3, waiting for transfers between devices, gathered_once(): both, at, found = (lax.all_gather(jnp.concatenate(lines), axis), 0, {})  230 us
    all_gather x1, waiting for transfers between devices, shards(): lax.all_gather(project(tokens, mem_key_w), 'head', axis=1, tiled=True)  61.9 us
    all_to_all x1, blocking collectives, sent_and_summed(): lax.all_to_all(split_up(value, dim, length), axis, 0, 0, tiled=True)  61.9 us
    all_gather x1, waiting for transfers between devices, shards(): lax.all_gather(2.0 / tok_rows * (predicted - value_share), 'head', axis=0...  57.5 us
    all_gather x1, waiting for transfers between devices, shards(): lax.all_gather(normalize(retrieved, norm_gain), 'head', axis=0, tiled=True)  54.4 us
    all_to_all x1, waiting for transfers between devices, sent_and_summed(): lax.all_to_all(split_up(value, dim, length), axis, 0, 0, tiled=True)  54.1 us
    ppermute x16, starting transfers between devices, shifted(): return lax.ppermute(value, axis, pairs)  50.5 us
    all_to_all x1, blocking collectives, sum_at_owner(): lax.all_to_all(split_up(value, dim, length), axis, 0, 0, tiled=True)  36.1 us
  transfers between devices with their start and end apart: 25, of which 10 were waited for; matrix products, arithmetic and copies ran while one was open for 6% of the time, Pallas kernels for 0%

profile of v1, /device:TPU:33, one launch (start us, length us, event | category | flops | bytes accessed | tf_op | source)
XLA Modules:
  0.0 774.1 jit_solution(9562553326930452772)
XLA Ops:
  9.8 61.9 %all-gather.14.cloned.1.call-done = bf16[512,1024]{1,0:T(8,128)(2,1)} async-done(((bf16[512,128]{1,0:T(8,128)(2,1)}), bf16[512,1024]{1,0:T(8,128)(2,1)}) %all-gather.14.cloned.1.call-update) | async-done | bytes 1048592 | tf_op jit(solution)/shard_map/all_gather | solution.py:200
  76.0 3.7 all-to-all-start.1
  81.0 54.1 %all-to-all-done.1 = f32[8,64,1024]{2,1,0:T(8,128)S(1)} async-done(((f32[8,64,1024]{2,1,0:T(8,128)}), f32[8,64,1024]{2,1,0:T(8,128)S(1)}, u32[]{:S(2)}, u32[]{:S(2)}) %all-to-all-start.1) | async-done | bytes 2097184 | tf_op jit(solution)/shard_map/all_to_all | solution.py:21
  135.3 23.0 %all-gather.16.cloned.1.call-done = bf16[512,1024]{1,0:T(8,128)(2,1)} async-done(((bf16[512,128]{1,0:T(8,128)(2,1)}), bf16[512,1024]{1,0:T(8,128)(2,1)}) %all-gather.16.cloned.1.call-update) | async-done | bytes 1048592 | tf_op jit(solution)/shard_map/all_gather | solution.py:201
  160.7 57.5 %all-gather.18.cloned.1.call-done = bf16[512,1024]{1,0:T(8,128)(2,1)} async-done(((bf16[64,1024]{1,0:T(8,128)(2,1)}), bf16[512,1024]{1,0:T(8,128)(2,1)}) %all-gather.18.cloned.1.call-update) | async-done | bytes 1048592 | tf_op jit(solution)/shard_map/all_gather | solution.py:208
  220.0 2.6 convolution_multiply_fusion
  222.7 4.1 concatenate.18
  226.8 17.6 %all-gather.22.cloned.1.call-done = f32[2,4099,128]{2,1,0:T(8,128)} async-done(((f32[1,4099,128]{2,1,0:T(8,128)}), f32[2,4099,128]{2,1,0:T(8,128)}) %all-gather.22.cloned.1.call-update) | async-done | bytes 4197392 | tf_op jit(solution)/shard_map/all_gather | solution.py:39
  251.5 4.1 concatenate.19
  255.6 154.2 %all-gather.24.cloned.1.call-done = f32[4,4099,128]{2,1,0:T(8,128)} async-done(((f32[1,4099,128]{2,1,0:T(8,128)}), f32[4,4099,128]{2,1,0:T(8,128)}) %all-gather.24.cloned.1.call-update) | async-done | bytes 8394768 | tf_op jit(solution)/shard_map/all_gather | solution.py:39
  418.9 4.0 bitcast_add_fusion
  423.0 4.1 concatenate.20
  428.8 6.5 all-to-all-start
  440.8 3.9 fusion.353
  453.9 58.6 %all-gather.26.cloned.1.call-done = f32[4,4099,128]{2,1,0:T(8,128)} async-done(((f32[1,4099,128]{2,1,0:T(8,128)}), f32[4,4099,128]{2,1,0:T(8,128)}) %all-gather.26.cloned.1.call-update) | async-done | bytes 8394768 | tf_op jit(solution)/shard_map/all_gather | solution.py:39
  512.4 3.5 fusion.352
  526.7 11.5 %fusion.57 = f32[512,1024]{1,0:T(8,128)} fusion(f32[128,1024]{1,0:T(8,128)} %squeeze.275, f32[128,1024]{1,0:T(8,128)} %squeeze.274, f32[128,1024]{1,0:T(8,128)} %squeeze.273, f32[128,1024]{1,0:T(8,128)} %squeeze.272, f32[128,1024]{1,0:T(8,128)} %squeeze.271, f32[128,1024]{1,0:T(8,128)} %squeeze.270, f32[128,1024]{1,0:T(8,128)} %squeeze.269, ...), kind=kOutput, calls=%fused_computation.101 | convolution fusion | flops 287834112 | bytes 25205248 | tf_op jit(solution)/shard_map/dot_general | solution.py:234
  538.1 61.9 %all_to_all.20 = f32[8,64,1024]{2,1,0:T(8,128)S(1)} all-to-all(f32[8,64,1024]{2,1,0:T(8,128)} %bitcast.564), channel_id=1, replica_groups=mesh['seq_0'=4,'seq_1'=4,'seq_2'=2,'head'=8] {'head'}, dimensions={0} | all-to-all | bytes 4194304 | tf_op jit(solution)/shard_map/all_to_all | solution.py:21
  601.5 54.4 %all-gather.20.cloned.1.call-done = bf16[512,1024]{1,0:T(8,128)(2,1)} async-done(((bf16[64,1024]{1,0:T(8,128)(2,1)}), bf16[512,1024]{1,0:T(8,128)(2,1)}) %all-gather.20.cloned.1.call-update) | async-done | bytes 1048592 | tf_op jit(solution)/shard_map/all_gather | solution.py:235
  657.6 3.1 collective-permute-start
  660.8 5.4 collective-permute-start.1
  666.2 3.6 collective-permute-start.2
  671.1 4.1 collective-permute-start.4
  677.4 3.0 collective-permute-start.5
  682.7 3.3 collective-permute-start.7
  688.8 8.3 %collective-permute-start.10 = (bf16[512,128]{1,0:T(8,128)(2,1)S(1)}, bf16[512,128]{1,0:T(8,128)(2,1)S(1)}, u32[]{:S(2)}, u32[]{:S(2)}) collective-permute-start(bf16[512,128]{1,0:T(8,128)(2,1)S(1)} %convolution_convert_fusion.1), channel_id=1, source_target_pairs={{0,48},{8,56},{16,64},{24,72},{32,80},{40,88},{48,96},{56,104},{64... | collective-permute-start | bytes 393224 | tf_op jit(solution)/shard_map/ppermute | solution.py:66
  697.1 2.8 collective-permute-start.11
  701.5 4.3 fusion.356
  705.8 4.2 fusion.355
  710.0 4.3 collective-permute-start.13
  716.4 3.0 collective-permute-start.15
  730.3 36.1 %all_to_all.21 = bf16[8,512,128]{2,1,0:T(8,128)(2,1)S(1)} all-to-all(bf16[8,512,128]{2,1,0:T(8,128)(2,1)S(1)} %bitcast.563), channel_id=1, replica_groups=mesh['seq_0'=4,'seq_1'=4,'seq_2'=2,'head'=8] {'head'}, dimensions={0} | all-to-all | bytes 2097152 | tf_op jit(solution)/shard_map/all_to_all | solution.py:71
  (203 shorter events, 82.4 us)
Async XLA Ops:
  6.5 67.7 %copy-start.14 = (f32[128,1024]{1,0:T(8,128)S(1)}, f32[128,1024]{1,0:T(8,128)}, u32[]{:S(2)}) copy-start(f32[128,1024]{1,0:T(8,128)} %param.20) | copy-start | bytes 1572868
  6.5 65.2 %all-gather.14.cloned.1.call-start = ((), (), s32[]{:S(2)}) async-start(), calls=%async_computation.4 | async-start | bytes 1179648 | tf_op jit(solution)/shard_map/all_gather | solution.py:200
  76.0 59.1 %all-to-all-start.1 = ((f32[8,64,1024]{2,1,0:T(8,128)}), f32[8,64,1024]{2,1,0:T(8,128)S(1)}, u32[]{:S(2)}, u32[]{:S(2)}) async-start(f32[8,64,1024]{2,1,0:T(8,128)} %bitcast.562), calls=%async_computation.1 | async-start | bytes 4194304 | tf_op jit(solution)/shard_map/all_to_all | solution.py:21
  79.7 80.9 %copy-start.21 = (f32[16,128]{1,0:T(8,128)S(1)}, f32[16,128]{1,0:T(8,128)}, u32[]{:S(2)}) copy-start(f32[16,128]{1,0:T(8,128)} %param.21) | copy-start | bytes 24580
  79.8 80.9 %copy-start.22 = (f32[16,128]{1,0:T(8,128)S(1)}, f32[16,128]{1,0:T(8,128)}, u32[]{:S(2)}) copy-start(f32[16,128]{1,0:T(8,128)} %param.22) | copy-start | bytes 24580
  79.8 80.9 %copy-start.23 = (f32[16,128]{1,0:T(8,128)S(1)}, f32[16,128]{1,0:T(8,128)}, u32[]{:S(2)}) copy-start(f32[16,128]{1,0:T(8,128)} %param.23) | copy-start | bytes 24580
  79.8 78.5 %all-gather.16.cloned.1.call-start = ((), (), s32[]{:S(2)}) async-start(), calls=%async_computation.5 | async-start | bytes 1179648 | tf_op jit(solution)/shard_map/all_gather | solution.py:201
  81.0 137.3 %all-gather.18.cloned.1.call-start = ((), (), s32[]{:S(2)}) async-start(), calls=%async_computation.6 | async-start | bytes 1179648 | tf_op jit(solution)/shard_map/all_gather | solution.py:208
  135.3 84.8 %copy-start.11 = (bf16[512,1024]{1,0:T(8,128)(2,1)S(1)}, bf16[512,1024]{1,0:T(8,128)(2,1)}, u32[]{:S(2)}) copy-start(bf16[512,1024]{1,0:T(8,128)(2,1)} %all-gather.14.cloned.1.call-done) | copy-start | bytes 3145732
  159.9 84.5 %all-gather.22.cloned.1.call-start = ((), (), s32[]{:S(2)}) async-start(), calls=%async_computation.8 | async-start | bytes 6303744 | tf_op jit(solution)/shard_map/all_gather | solution.py:39
  226.8 183.1 %all-gather.24.cloned.1.call-start = ((), (), s32[]{:S(2)}) async-start(), calls=%async_computation.9 | async-start | bytes 10506240 | tf_op jit(solution)/shard_map/all_gather | solution.py:39
  255.6 256.9 %all-gather.26.cloned.1.call-start = ((), (), s32[]{:S(2)}) async-start(), calls=%async_computation.10 | async-start | bytes 10506240 | tf_op jit(solution)/shard_map/all_gather | solution.py:39
  428.8 97.9 %all-to-all-start = ((bf16[8,512,128]{1,2,0:T(8,128)(2,1)}), bf16[8,512,128]{1,2,0:T(8,128)(2,1)}, u32[]{:S(2)}, u32[]{:S(2)}) async-start(bf16[8,512,128]{1,2,0:T(8,128)(2,1)} %stack.2), calls=%async_computation | async-start | bytes 2097152 | tf_op jit(solution)/shard_map/all_to_all | solution.py:196
  435.2 220.6 %all-gather.20.cloned.1.call-start = ((), (), s32[]{:S(2)}) async-start(), calls=%async_computation.7 | async-start | bytes 1179648 | tf_op jit(solution)/shard_map/all_gather | solution.py:235
  600.2 75.0 %copy-start.18 = (bf16[1024,128]{1,0:T(8,128)(2,1)S(1)}, bf16[1024,128]{1,0:T(8,128)(2,1)}, u32[]{:S(2)}) copy-start(bf16[1024,128]{1,0:T(8,128)(2,1)} %param.26) | copy-start | bytes 786436
  600.2 76.7 %copy-start.19 = (bf16[1024,128]{1,0:T(8,128)(2,1)S(1)}, bf16[1024,128]{1,0:T(8,128)(2,1)}, u32[]{:S(2)}) copy-start(bf16[1024,128]{1,0:T(8,128)(2,1)} %param.28) | copy-start | bytes 786436
  657.6 19.7 %collective-permute-start = (bf16[512,128]{1,0:T(8,128)(2,1)S(1)}, bf16[512,128]{1,0:T(8,128)(2,1)S(1)}, u32[]{:S(2)}, u32[]{:S(2)}) collective-permute-start(bf16[512,128]{1,0:T(8,128)(2,1)S(1)} %convolution_convert_fusion.2), channel_id=1, source_target_pairs={{0,64},{8,72},{16,80},{24,88},{32,96},{40,104},{48,112},{56,120},{... | collective-permute-start | bytes 393224 | tf_op jit(solution)/shard_map/ppermute | solution.py:66
  660.8 19.7 %collective-permute-start.1 = (bf16[512,128]{1,0:T(8,128)(2,1)S(1)}, bf16[512,128]{1,0:T(8,128)(2,1)S(1)}, u32[]{:S(2)}, u32[]{:S(2)}) collective-permute-start(bf16[512,128]{1,0:T(8,128)(2,1)S(1)} %convolution_convert_fusion.2), channel_id=1, source_target_pairs={{0,56},{8,64},{16,72},{24,80},{32,88},{40,96},{48,104},{56,112},{6... | collective-permute-start | bytes 393224 | tf_op jit(solution)/shard_map/ppermute | solution.py:66
  666.2 16.6 %collective-permute-start.2 = (bf16[512,128]{1,0:T(8,128)(2,1)S(1)}, bf16[512,128]{1,0:T(8,128)(2,1)S(1)}, u32[]{:S(2)}, u32[]{:S(2)}) collective-permute-start(bf16[512,128]{1,0:T(8,128)(2,1)S(1)} %convolution_convert_fusion.2), channel_id=1, source_target_pairs={{0,48},{8,56},{16,64},{24,72},{32,80},{40,88},{48,96},{56,104},{64... | collective-permute-start | bytes 393224 | tf_op jit(solution)/shard_map/ppermute | solution.py:66
  669.8 16.3 %collective-permute-start.3 = (bf16[512,128]{1,0:T(8,128)(2,1)S(1)}, bf16[512,128]{1,0:T(8,128)(2,1)S(1)}, u32[]{:S(2)}, u32[]{:S(2)}) collective-permute-start(bf16[512,128]{1,0:T(8,128)(2,1)S(1)} %convolution_convert_fusion.2), channel_id=1, source_target_pairs={{0,40},{8,48},{16,56},{24,64},{32,72},{40,80},{48,88},{56,96},{64,... | collective-permute-start | bytes 393224 | tf_op jit(solution)/shard_map/ppermute | solution.py:66
  671.1 16.3 %collective-permute-start.4 = (bf16[512,128]{1,0:T(8,128)(2,1)S(1)}, bf16[512,128]{1,0:T(8,128)(2,1)S(1)}, u32[]{:S(2)}, u32[]{:S(2)}) collective-permute-start(bf16[512,128]{1,0:T(8,128)(2,1)S(1)} %convolution_convert_fusion.2), channel_id=1, source_target_pairs={{0,32},{8,40},{16,48},{24,56},{32,64},{40,72},{48,80},{56,88},{64,... | collective-permute-start | bytes 393224 | tf_op jit(solution)/shard_map/ppermute | solution.py:66
  677.4 11.4 %collective-permute-start.5 = (bf16[512,128]{1,0:T(8,128)(2,1)S(1)}, bf16[512,128]{1,0:T(8,128)(2,1)S(1)}, u32[]{:S(2)}, u32[]{:S(2)}) collective-permute-start(bf16[512,128]{1,0:T(8,128)(2,1)S(1)} %convolution_convert_fusion.2), channel_id=1, source_target_pairs={{0,24},{8,32},{16,40},{24,48},{32,56},{40,64},{48,72},{56,80},{64,... | collective-permute-start | bytes 393224 | tf_op jit(solution)/shard_map/ppermute | solution.py:66
  680.4 16.6 %collective-permute-start.6 = (bf16[512,128]{1,0:T(8,128)(2,1)S(1)}, bf16[512,128]{1,0:T(8,128)(2,1)S(1)}, u32[]{:S(2)}, u32[]{:S(2)}) collective-permute-start(bf16[512,128]{1,0:T(8,128)(2,1)S(1)} %convolution_convert_fusion.2), channel_id=1, source_target_pairs={{0,16},{8,24},{16,32},{24,40},{32,48},{40,56},{48,64},{56,72},{64,... | collective-permute-start | bytes 393224 | tf_op jit(solution)/shard_map/ppermute | solution.py:66
  682.7 17.2 %collective-permute-start.7 = (bf16[512,128]{1,0:T(8,128)(2,1)S(1)}, bf16[512,128]{1,0:T(8,128)(2,1)S(1)}, u32[]{:S(2)}, u32[]{:S(2)}) collective-permute-start(bf16[512,128]{1,0:T(8,128)(2,1)S(1)} %convolution_convert_fusion.2), channel_id=1, source_target_pairs={{0,8},{8,16},{16,24},{24,32},{32,40},{40,48},{48,56},{56,64},{64,7... | collective-permute-start | bytes 393224 | tf_op jit(solution)/shard_map/ppermute | solution.py:66
  686.1 23.9 %collective-permute-start.8 = (bf16[512,128]{1,0:T(8,128)(2,1)S(1)}, bf16[512,128]{1,0:T(8,128)(2,1)S(1)}, u32[]{:S(2)}, u32[]{:S(2)}) collective-permute-start(bf16[512,128]{1,0:T(8,128)(2,1)S(1)} %convolution_convert_fusion.1), channel_id=1, source_target_pairs={{0,64},{8,72},{16,80},{24,88},{32,96},{40,104},{48,112},{56,120},{... | collective-permute-start | bytes 393224 | tf_op jit(solution)/shard_map/ppermute | solution.py:66
  687.4 26.9 %collective-permute-start.9 = (bf16[512,128]{1,0:T(8,128)(2,1)S(1)}, bf16[512,128]{1,0:T(8,128)(2,1)S(1)}, u32[]{:S(2)}, u32[]{:S(2)}) collective-permute-start(bf16[512,128]{1,0:T(8,128)(2,1)S(1)} %convolution_convert_fusion.1), channel_id=1, source_target_pairs={{0,56},{8,64},{16,72},{24,80},{32,88},{40,96},{48,104},{56,112},{6... | collective-permute-start | bytes 393224 | tf_op jit(solution)/shard_map/ppermute | solution.py:66
  688.8 27.6 %collective-permute-start.10 = (bf16[512,128]{1,0:T(8,128)(2,1)S(1)}, bf16[512,128]{1,0:T(8,128)(2,1)S(1)}, u32[]{:S(2)}, u32[]{:S(2)}) collective-permute-start(bf16[512,128]{1,0:T(8,128)(2,1)S(1)} %convolution_convert_fusion.1), channel_id=1, source_target_pairs={{0,48},{8,56},{16,64},{24,72},{32,80},{40,88},{48,96},{56,104},{64... | collective-permute-start | bytes 393224 | tf_op jit(solution)/shard_map/ppermute | solution.py:66
  697.1 22.3 %collective-permute-start.11 = (bf16[512,128]{1,0:T(8,128)(2,1)S(1)}, bf16[512,128]{1,0:T(8,128)(2,1)S(1)}, u32[]{:S(2)}, u32[]{:S(2)}) collective-permute-start(bf16[512,128]{1,0:T(8,128)(2,1)S(1)} %convolution_convert_fusion.1), channel_id=1, source_target_pairs={{0,40},{8,48},{16,56},{24,64},{32,72},{40,80},{48,88},{56,96},{64,... | collective-permute-start | bytes 393224 | tf_op jit(solution)/shard_map/ppermute | solution.py:66
  699.9 19.6 %collective-permute-start.12 = (bf16[512,128]{1,0:T(8,128)(2,1)S(1)}, bf16[512,128]{1,0:T(8,128)(2,1)S(1)}, u32[]{:S(2)}, u32[]{:S(2)}) collective-permute-start(bf16[512,128]{1,0:T(8,128)(2,1)S(1)} %convolution_convert_fusion.1), channel_id=1, source_target_pairs={{0,32},{8,40},{16,48},{24,56},{32,64},{40,72},{48,80},{56,88},{64,... | collective-permute-start | bytes 393224 | tf_op jit(solution)/shard_map/ppermute | solution.py:66
  710.0 9.5 %collective-permute-start.13 = (bf16[512,128]{1,0:T(8,128)(2,1)S(1)}, bf16[512,128]{1,0:T(8,128)(2,1)S(1)}, u32[]{:S(2)}, u32[]{:S(2)}) collective-permute-start(bf16[512,128]{1,0:T(8,128)(2,1)S(1)} %convolution_convert_fusion.1), channel_id=1, source_target_pairs={{0,24},{8,32},{16,40},{24,48},{32,56},{40,64},{48,72},{56,80},{64,... | collective-permute-start | bytes 393224 | tf_op jit(solution)/shard_map/ppermute | solution.py:66
  714.4 6.9 collective-permute-start.14
  716.4 6.2 collective-permute-start.15
  (18 other events, 234.5 us)
Sparse Core Ops, SparseCore 0:
  9.9 61.7 all-gather.13
  83.1 75.1 all-gather.15
  160.9 57.3 all-gather.17
  226.9 17.4 all-gather.21
  255.7 154.1 all-gather.23
  427.2 85.1 all-gather.25
  601.6 54.2 all-gather.19
